TPU v7x, 32 devices: a whole 2x2x4 slice. The times are simulated.
32 devices in a mesh: tm: 16 (over z, y, x), rows: 2 (over core).
Axes of the slice: x: 2, y: 2, z: 4, core: 2. Of those that a mesh axis runs over, the one named last changes fastest.
Arguments:
- resid: float32 [2, 16, 16, 512], P(None, 'tm', 'rows'), may hold values from -3 to 3
- basis: float32 [4, 2, 16, 16, 512], P(None, None, 'tm', 'rows'), may hold values from -0.01171875 to 0.01171875
Outputs:
- precond: float32 [2, 16, 16, 512], P(None, 'tm', 'rows')
- image: float32 [2, 16, 16, 512], P(None, 'tm', 'rows')
- gram: float32 [5], replicated
All inputs are finite; a program needn't handle non-finite values.
Results may differ from a plain program's by a relative error of at most 0.0005.
Values sent between devices are 32-bit elements; how exact they have to be, the bound alone decides.
A program may use at most 64 MiB of HBM per device.

v0:
```python
import math
import jax
import jax.numpy as jnp
from jax import lax
from jax.sharding import PartitionSpec as P

SWEEPS = 4
ALPHA = 0.01


def padded_2(shard, sides, width):
    for axis, dim in sides:
        count, length = (lax.axis_size(axis), shard.shape[dim])
        up = [(i, (i + 1) % count) for i in range(count - 1)]
        down = [(j, i) for i, j in up]
        last = lax.slice_in_dim(shard, length - width, length, axis=dim)
        first = lax.slice_in_dim(shard, 0, width, axis=dim)
        before = lax.ppermute(last, axis, up)
        after = lax.ppermute(first, axis, down)
        shard = jnp.concatenate([before, shard, after], axis=dim)
    return shard


def shifted(value, axis, steps):
    count = lax.axis_size(axis)
    first, last = (max(0, -steps), min(count, count - steps))
    return lax.ppermute(value, axis, [(source, source + steps) for source in range(first, last)])


def neighbours(padded):
    middle = padded[:, 1:-1]
    sides = jnp.pad(middle, ((0, 0), (0, 0), (1, 1)))
    return padded[:, 2:] + padded[:, :-2] + sides[:, :, 2:] + sides[:, :, :-2]


def cmul(left, right_re, right_im):
    return jnp.stack(
        [left[0] * right_re - left[1] * right_im, left[0] * right_im + left[1] * right_re]
    )


def phases(first, second, steps):
    turns = first * second % steps
    angle = turns.astype(jnp.float32) * (2.0 * math.pi / steps)
    return (jnp.cos(angle), jnp.sin(angle))


def on_device(resid, basis):
    steps = lax.axis_size("tm")
    coupling = 16.0 / (steps * steps)
    me = lax.axis_index("tm")
    rows_dev = resid.shape[2]
    cols = resid.shape[3]
    cells = rows_dev * cols
    piece = cells // steps
    mine = me.astype(jnp.float32)
    gamma = jnp.power(jnp.float32(ALPHA), mine / steps)
    scaled = resid[:, 0] * gamma
    ordinal = jnp.arange(steps, dtype=jnp.int32)
    cos_table, sin_table = phases(ordinal[:, None], ordinal[None, :], steps)
    blocks = lax.all_to_all(
        scaled.reshape(1, 2, cells), "tm", split_axis=2, concat_axis=0, tiled=True
    )
    flat = blocks.reshape(steps, 2 * piece)
    real_part = jnp.dot(cos_table, flat, precision=lax.Precision.HIGHEST)
    imag_part = -jnp.dot(sin_table, flat, precision=lax.Precision.HIGHEST)
    stacked = jnp.stack([real_part, imag_part], 1).reshape(steps, 2, 2, piece)
    spectrum = lax.all_to_all(stacked, "tm", split_axis=0, concat_axis=3, tiled=True)
    rhat = spectrum[0].reshape(2, 2, rows_dev, cols)
    base = jnp.power(jnp.float32(ALPHA), jnp.float32(1.0) / steps)
    angle = mine * (2.0 * math.pi / steps)
    lam_re = 1.0 - base * jnp.cos(angle)
    lam_im = base * jnp.sin(angle)
    disp_spec = rhat[:, 0]
    right = cmul(disp_spec, lam_re, lam_im) + rhat[:, 1]
    den_re = lam_re * lam_re - lam_im * lam_im + 4.0 * coupling
    den_im = 2.0 * lam_re * lam_im
    magnitude = den_re * den_re + den_im * den_im
    inv_re = den_re / magnitude
    inv_im = -den_im / magnitude
    uhat = cmul(right, inv_re, inv_im)
    for sweep in range(SWEEPS - 1):
        padded = padded_2(uhat, (("rows", 1),), 1)
        uhat = cmul(right + coupling * neighbours(padded), inv_re, inv_im)
    vhat = cmul(uhat, lam_re, lam_im) - disp_spec
    yhat = jnp.stack([uhat, vhat], 1)
    spread = lax.all_to_all(
        yhat.reshape(1, 2, 2, cells), "tm", split_axis=3, concat_axis=0, tiled=True
    )
    real_rows = spread[:, 0].reshape(steps, 2 * piece)
    imag_rows = spread[:, 1].reshape(steps, 2 * piece)
    undo = jnp.power(jnp.float32(ALPHA), -ordinal.astype(jnp.float32) / steps) / steps
    history = jnp.dot(cos_table, real_rows, precision=lax.Precision.HIGHEST) - jnp.dot(
        sin_table, imag_rows, precision=lax.Precision.HIGHEST
    )
    history = (history * undo[:, None]).reshape(steps, 2, piece)
    returned = lax.all_to_all(history, "tm", split_axis=0, concat_axis=2, tiled=True)
    precond = returned[0].reshape(2, rows_dev, cols)
    earlier = shifted(precond, "tm", 1)
    disp_rim = padded_2(precond[0:1], (("rows", 1),), 1)
    laplace = neighbours(disp_rim)[0] - 4.0 * precond[0]
    first = precond[0] - earlier[0] - precond[1]
    second = precond[1] - earlier[1] - coupling * laplace
    image = jnp.stack([first, second])
    inner = jnp.sum(basis[:, :, 0] * image[None], axis=(1, 2, 3))
    count = 2.0 * steps * rows_dev * lax.axis_size("rows") * cols
    squares = jnp.sum(image * image) / count
    local_terms = jnp.concatenate([inner, squares[None]])
    gram = lax.psum(local_terms, ("tm", "rows"))
    return (precond[:, None], image[:, None], gram)


def solution(mesh):
    in_specs = (P(None, "tm", "rows", None), P(None, None, "tm", "rows", None))
    out_specs = (P(None, "tm", "rows", None), P(None, "tm", "rows", None), P())
    return jax.shard_map(
        on_device, mesh=mesh, in_specs=in_specs, out_specs=out_specs, check_vma=False
    )
```

profile of v0, /device:TPU:0, one launch (start us, length us, event | category | flops | bytes accessed | tf_op | source)
XLA Modules:
  0.0 169.4 jit_solution(10434036143663607024)
XLA Ops:
  2.6 19.4 %reduce.4 = f32[4096,2]{1,0:T(8,128)} reduce(f32[4096,1,2]{2,1,0:T(1,128)S(1)} %bitcast.83, f32[]{:T(128)} %broadcast.139), dimensions={1}, to_apply=%bitcast.65.reduce_sub_computation | reduce | bytes 65540
  22.0 3.0 %reshape.138 = f32[16,1,512]{2,1,0:T(1,128)S(1)} reshape(f32[4096,2]{1,0:T(8,128)} %reduce.4) | data formatting | bytes 65536
  25.0 15.5 %all_to_all.63 = f32[16,1,512]{2,1,0:T(1,128)S(1)} all-to-all(f32[16,1,512]{2,1,0:T(1,128)S(1)} %reshape.138), channel_id=1, replica_groups=mesh['tm'=16,'rows'=2] {'tm'}, dimensions={0} | all-to-all | bytes 65536 | tf_op jit(solution)/shard_map/all_to_all | solution.py:61
  41.3 3.4 %reshape.139 = f32[4096,1,2]{2,1,0:T(1,128)S(1)} reshape(f32[16,512]{1,0:T(8,128)S(1)} %reduce.5) | data formatting | bytes 65536
  46.5 3.5 %all-to-all-start.1 = ((f32[16,2,2,256]{3,2,1,0:T(2,128)}), f32[16,2,2,256]{3,2,1,0:T(2,128)S(1)}, u32[]{:S(2)}, u32[]{:S(2)}) async-start(f32[16,2,2,256]{3,2,1,0:T(2,128)} %copy.48), calls=%async_computation.1 | async-start | bytes 131072 | tf_op jit(solution)/shard_map/all_to_all | solution.py:68
  50.2 7.2 %all-to-all-done.1 = f32[16,2,2,256]{3,2,1,0:T(2,128)S(1)} async-done(((f32[16,2,2,256]{3,2,1,0:T(2,128)}), f32[16,2,2,256]{3,2,1,0:T(2,128)S(1)}, u32[]{:S(2)}, u32[]{:S(2)}) %all-to-all-start.1) | async-done | bytes 65568 | tf_op jit(solution)/shard_map/all_to_all | solution.py:68
  57.6 1.3 collective-permute-start
  58.9 3.0 %collective-permute-start.1 = (f32[2,1,512]{2,1,0:T(1,128)S(1)}, f32[2,1,512]{2,1,0:T(1,128)S(1)}, u32[]{:S(2)}, u32[]{:S(2)}) collective-permute-start(f32[2,1,512]{2,1,0:T(1,128)S(1)} %get-tuple-element.26), channel_id=1, source_target_pairs={{0,1},{2,3},{4,5},{6,7},{8,9},{10,11},{12,13},{14,15},{16,17},{18,... | collective-permute-start | bytes 12296 | tf_op jit(solution)/shard_map/ppermute | solution.py:18
  62.9 1.3 collective-permute-start.2
  64.2 3.0 %collective-permute-start.3 = (f32[2,1,512]{2,1,0:T(1,128)S(1)}, f32[2,1,512]{2,1,0:T(1,128)S(1)}, u32[]{:S(2)}, u32[]{:S(2)}) collective-permute-start(f32[2,1,512]{2,1,0:T(1,128)S(1)} %get-tuple-element.22), channel_id=1, source_target_pairs={{0,1},{2,3},{4,5},{6,7},{8,9},{10,11},{12,13},{14,15},{16,17},{18,... | collective-permute-start | bytes 12296 | tf_op jit(solution)/shard_map/ppermute | solution.py:18
  68.1 1.3 collective-permute-start.4
  69.4 3.2 %collective-permute-start.5 = (f32[2,1,512]{2,1,0:T(1,128)S(1)}, f32[2,1,512]{2,1,0:T(1,128)S(1)}, u32[]{:S(2)}, u32[]{:S(2)}) collective-permute-start(f32[2,1,512]{2,1,0:T(1,128)S(1)} %get-tuple-element.18), channel_id=1, source_target_pairs={{0,1},{2,3},{4,5},{6,7},{8,9},{10,11},{12,13},{14,15},{16,17},{18,... | collective-permute-start | bytes 12296 | tf_op jit(solution)/shard_map/ppermute | solution.py:18
  73.5 4.4 %copy.51 = f32[1,2,2,4096]{2,1,0,3:T(2,128)} copy(f32[1,2,2,4096]{3,1,2,0:T(2,128)S(1)} %pad_maximum_fusion.1) | data formatting | bytes 131072 | tf_op jit(solution)/shard_map/stack | solution.py:86
  77.9 8.1 %reshape.140 = f32[16,1,1024]{2,1,0:T(1,128)} reshape(f32[4096,1,2,2]{3,2,1,0:T(2,128)} %bitcast.81) | data formatting | bytes 131072
  86.0 3.5 %all-to-all-start.2 = ((f32[16,1,1024]{2,1,0:T(1,128)}), f32[16,1,1024]{2,1,0:T(1,128)S(1)}, u32[]{:S(2)}, u32[]{:S(2)}) async-start(f32[16,1,1024]{2,1,0:T(1,128)} %reshape.140), calls=%async_computation.2 | async-start | bytes 131072 | tf_op jit(solution)/shard_map/all_to_all | solution.py:87
  89.5 7.5 %all-to-all-done.2 = f32[16,1,1024]{2,1,0:T(1,128)S(1)} async-done(((f32[16,1,1024]{2,1,0:T(1,128)}), f32[16,1,1024]{2,1,0:T(1,128)S(1)}, u32[]{:S(2)}, u32[]{:S(2)}) %all-to-all-start.2) | async-done | bytes 65568 | tf_op jit(solution)/shard_map/all_to_all | solution.py:87
  97.8 7.7 %reshape.141 = f32[4096,1,2,2]{3,2,1,0:T(2,128)} reshape(f32[16,1024]{1,0:T(8,128)S(1)} %reduce.6) | data formatting | bytes 131072
  105.6 3.6 %copy.57 = f32[1,2,2,16,256]{4,3,2,1,0:T(8,128)S(1)} copy(f32[1,2,2,16,256]{2,1,4,3,0:T(2,128)} %bitcast.82) | data formatting | bytes 131072 | tf_op jit(solution)/shard_map/all_to_all | solution.py:87
  109.7 10.0 %all_to_all.64 = f32[16,2,256]{2,1,0:T(2,128)S(1)} all-to-all(f32[16,2,256]{2,1,0:T(2,128)S(1)} %reshape.134), channel_id=1, replica_groups=mesh['tm'=16,'rows'=2] {'tm'}, dimensions={0} | all-to-all | bytes 65536 | tf_op jit(solution)/shard_map/all_to_all | solution.py:97
  119.8 2.6 %collective-permute-start.6 = (f32[2,8,512]{2,1,0:T(8,128)S(1)}, f32[2,8,512]{2,1,0:T(8,128)S(1)}, u32[]{:S(2)}, u32[]{:S(2)}) collective-permute-start(f32[2,8,512]{2,1,0:T(8,128)S(1)} %reshape_squeeze.15), channel_id=1, source_target_pairs={{0,2},{2,4},{4,6},{6,8},{8,10},{10,12},{12,14},{14,16},{16,18},{18... | collective-permute-start | bytes 98312 | tf_op jit(solution)/shard_map/ppermute | solution.py:27
  122.4 1.3 collective-permute-start.7
  123.7 3.0 %collective-permute-start.8 = (f32[1,1,512]{2,1,0:T(1,128)S(1)}, f32[1,1,512]{2,1,0:T(1,128)S(1)}, u32[]{:S(2)}, u32[]{:S(2)}) collective-permute-start(f32[1,1,512]{2,1,0:T(1,128)S(1)} %get-tuple-element.30), channel_id=1, source_target_pairs={{0,1},{2,3},{4,5},{6,7},{8,9},{10,11},{12,13},{14,15},{16,17},{18,... | collective-permute-start | bytes 6152 | tf_op jit(solution)/shard_map/ppermute | solution.py:18
  127.7 1.2 pad_maximum_fusion.18
  130.4 39.0 %psum.7 = f32[5]{0:T(128)} all-reduce(f32[5]{0:T(128)S(1)} %pad_maximum_fusion.21), channel_id=1, replica_groups=mesh['tm'=16,'rows'=2] {'tm','rows'}, use_global_device_ids=true, to_apply=%region_2.3 | all-reduce | flops 5 | bytes 40 | tf_op jit(solution)/shard_map/psum | solution.py:109
  (66 shorter events, 10.2 us)
Async XLA Ops:
  46.5 11.0 %all-to-all-start.1 = ((f32[16,2,2,256]{3,2,1,0:T(2,128)}), f32[16,2,2,256]{3,2,1,0:T(2,128)S(1)}, u32[]{:S(2)}, u32[]{:S(2)}) async-start(f32[16,2,2,256]{3,2,1,0:T(2,128)} %copy.48), calls=%async_computation.1 | async-start | bytes 131072 | tf_op jit(solution)/shard_map/all_to_all | solution.py:68
  57.6 4.3 %collective-permute-start = (f32[2,1,512]{2,1,0:T(1,128)S(1)}, f32[2,1,512]{2,1,0:T(1,128)S(1)}, u32[]{:S(2)}, u32[]{:S(2)}) collective-permute-start(f32[2,1,512]{2,1,0:T(1,128)S(1)} %get-tuple-element.25), channel_id=1, source_target_pairs={{1,0},{3,2},{5,4},{7,6},{9,8},{11,10},{13,12},{15,14},{17,16},{19,... | collective-permute-start | bytes 12296 | tf_op jit(solution)/shard_map/ppermute | solution.py:19
  58.9 3.8 %collective-permute-start.1 = (f32[2,1,512]{2,1,0:T(1,128)S(1)}, f32[2,1,512]{2,1,0:T(1,128)S(1)}, u32[]{:S(2)}, u32[]{:S(2)}) collective-permute-start(f32[2,1,512]{2,1,0:T(1,128)S(1)} %get-tuple-element.26), channel_id=1, source_target_pairs={{0,1},{2,3},{4,5},{6,7},{8,9},{10,11},{12,13},{14,15},{16,17},{18,... | collective-permute-start | bytes 12296 | tf_op jit(solution)/shard_map/ppermute | solution.py:18
  62.9 4.3 %collective-permute-start.2 = (f32[2,1,512]{2,1,0:T(1,128)S(1)}, f32[2,1,512]{2,1,0:T(1,128)S(1)}, u32[]{:S(2)}, u32[]{:S(2)}) collective-permute-start(f32[2,1,512]{2,1,0:T(1,128)S(1)} %get-tuple-element.21), channel_id=1, source_target_pairs={{1,0},{3,2},{5,4},{7,6},{9,8},{11,10},{13,12},{15,14},{17,16},{19,... | collective-permute-start | bytes 12296 | tf_op jit(solution)/shard_map/ppermute | solution.py:19
  64.2 3.8 %collective-permute-start.3 = (f32[2,1,512]{2,1,0:T(1,128)S(1)}, f32[2,1,512]{2,1,0:T(1,128)S(1)}, u32[]{:S(2)}, u32[]{:S(2)}) collective-permute-start(f32[2,1,512]{2,1,0:T(1,128)S(1)} %get-tuple-element.22), channel_id=1, source_target_pairs={{0,1},{2,3},{4,5},{6,7},{8,9},{10,11},{12,13},{14,15},{16,17},{18,... | collective-permute-start | bytes 12296 | tf_op jit(solution)/shard_map/ppermute | solution.py:18
  68.1 4.5 %collective-permute-start.4 = (f32[2,1,512]{2,1,0:T(1,128)S(1)}, f32[2,1,512]{2,1,0:T(1,128)S(1)}, u32[]{:S(2)}, u32[]{:S(2)}) collective-permute-start(f32[2,1,512]{2,1,0:T(1,128)S(1)} %get-tuple-element.17), channel_id=1, source_target_pairs={{1,0},{3,2},{5,4},{7,6},{9,8},{11,10},{13,12},{15,14},{17,16},{19,... | collective-permute-start | bytes 12296 | tf_op jit(solution)/shard_map/ppermute | solution.py:19
  69.4 3.8 %collective-permute-start.5 = (f32[2,1,512]{2,1,0:T(1,128)S(1)}, f32[2,1,512]{2,1,0:T(1,128)S(1)}, u32[]{:S(2)}, u32[]{:S(2)}) collective-permute-start(f32[2,1,512]{2,1,0:T(1,128)S(1)} %get-tuple-element.18), channel_id=1, source_target_pairs={{0,1},{2,3},{4,5},{6,7},{8,9},{10,11},{12,13},{14,15},{16,17},{18,... | collective-permute-start | bytes 12296 | tf_op jit(solution)/shard_map/ppermute | solution.py:18
  86.0 11.0 %all-to-all-start.2 = ((f32[16,1,1024]{2,1,0:T(1,128)}), f32[16,1,1024]{2,1,0:T(1,128)S(1)}, u32[]{:S(2)}, u32[]{:S(2)}) async-start(f32[16,1,1024]{2,1,0:T(1,128)} %reshape.140), calls=%async_computation.2 | async-start | bytes 131072 | tf_op jit(solution)/shard_map/all_to_all | solution.py:87
  105.6 24.0 %copy-start = (f32[4,2,1,8,512]{4,3,2,1,0:T(8,128)S(1)}, f32[4,2,1,8,512]{4,3,2,1,0:T(8,128)}, u32[]{:S(2)}) copy-start(f32[4,2,1,8,512]{4,3,2,1,0:T(8,128)} %param.3) | copy-start | bytes 393220
  119.8 7.8 %collective-permute-start.6 = (f32[2,8,512]{2,1,0:T(8,128)S(1)}, f32[2,8,512]{2,1,0:T(8,128)S(1)}, u32[]{:S(2)}, u32[]{:S(2)}) collective-permute-start(f32[2,8,512]{2,1,0:T(8,128)S(1)} %reshape_squeeze.15), channel_id=1, source_target_pairs={{0,2},{2,4},{4,6},{6,8},{8,10},{10,12},{12,14},{14,16},{16,18},{18... | collective-permute-start | bytes 98312 | tf_op jit(solution)/shard_map/ppermute | solution.py:27
  122.4 4.4 %collective-permute-start.7 = (f32[1,1,512]{2,1,0:T(1,128)S(1)}, f32[1,1,512]{2,1,0:T(1,128)S(1)}, u32[]{:S(2)}, u32[]{:S(2)}) collective-permute-start(f32[1,1,512]{2,1,0:T(1,128)S(1)} %get-tuple-element.29), channel_id=1, source_target_pairs={{1,0},{3,2},{5,4},{7,6},{9,8},{11,10},{13,12},{15,14},{17,16},{19,... | collective-permute-start | bytes 6152 | tf_op jit(solution)/shard_map/ppermute | solution.py:19
  123.7 3.8 %collective-permute-start.8 = (f32[1,1,512]{2,1,0:T(1,128)S(1)}, f32[1,1,512]{2,1,0:T(1,128)S(1)}, u32[]{:S(2)}, u32[]{:S(2)}) collective-permute-start(f32[1,1,512]{2,1,0:T(1,128)S(1)} %get-tuple-element.30), channel_id=1, source_target_pairs={{0,1},{2,3},{4,5},{6,7},{8,9},{10,11},{12,13},{14,15},{16,17},{18,... | collective-permute-start | bytes 6152 | tf_op jit(solution)/shard_map/ppermute | solution.py:18
where the time goes:
time: 170 us; the launch traced here: 169 us
  blocking collectives  64.5 us (38%)
  local copies, waits for them, and re-layouts  33.7 us (20%)
  starting transfers between devices  27 us (16%)
  other arithmetic  23.6 us (14%)
  waiting for transfers between devices  17.7 us (10%)
  between operations  2.06 us (1%)
    psum x1, blocking collectives, on_device(): gram = lax.psum(local_terms, ('tm', 'rows'))  39 us
    unnamed x10, local copies, waits for them, and re-layouts  22.8 us
    unnamed x1, other arithmetic  19.4 us
    all_to_all x1, blocking collectives, on_device(): lax.all_to_all(scaled.reshape(1, 2, cells), 'tm', split_axis=2, concat_ax...  15.5 us
    ppermute x4, starting transfers between devices, padded_2(): before = lax.ppermute(last, axis, up)  12.3 us
    all_to_all x1, blocking collectives, on_device(): lax.all_to_all(history, 'tm', split_axis=0, concat_axis=2, tiled=True)  9.98 us
    all_to_all x1, waiting for transfers between devices, on_device(): lax.all_to_all(yhat.reshape(1, 2, 2, cells), 'tm', split_axis=3, concat_a...  7.49 us
    all_to_all x1, waiting for transfers between devices, on_device(): lax.all_to_all(stacked, 'tm', split_axis=0, concat_axis=3, tiled=True)  7.25 us
  transfers between devices with their start and end apart: 11, of which 6 were waited for; matrix products, arithmetic and copies ran while one was open for 0% of the time, Pallas kernels for 0%

commit v1 on v0

--- a/solution.py
+++ b/solution.py
@@ -94,7 +94,10 @@
         sin_table, imag_rows, precision=lax.Precision.HIGHEST
     )
     history = (history * undo[:, None]).reshape(steps, 2, piece)
-    returned = lax.all_to_all(history, "tm", split_axis=0, concat_axis=2, tiled=True)
+    returned = jnp.concatenate(
+        lax.all_to_all(jnp.stack(jnp.split(history, lax.axis_size("tm"), axis=0)), "tm", 0, 0),
+        axis=2,
+    )
     precond = returned[0].reshape(2, rows_dev, cols)
     earlier = shifted(precond, "tm", 1)
     disp_rim = padded_2(precond[0:1], (("rows", 1),), 1)

time: 170 us -> 171 us (level)
    unnamed x10 -> x25, local copies, waits for them, and re-layouts: 22.8 us -> 22.9 us
where the time goes in v1:
time: 171 us; the launch traced here: 170 us
  blocking collectives  64.5 us (38%)
  local copies, waits for them, and re-layouts  34.1 us (20%)
  starting transfers between devices  27 us (16%)
  other arithmetic  23.6 us (14%)
  waiting for transfers between devices  17.7 us (10%)
  between operations  2.1 us (1%)
    psum x1, blocking collectives, on_device(): gram = lax.psum(local_terms, ('tm', 'rows'))  39 us
    unnamed x25, local copies, waits for them, and re-layouts  22.9 us
    unnamed x1, other arithmetic  19.4 us
    all_to_all x1, blocking collectives, on_device(): lax.all_to_all(scaled.reshape(1, 2, cells), 'tm', split_axis=2, concat_ax...  15.5 us
    ppermute x4, starting transfers between devices, padded_2(): before = lax.ppermute(last, axis, up)  12.3 us
    all_to_all x1, blocking collectives, on_device(): lax.all_to_all(jnp.stack(jnp.split(history, lax.axis_size('tm'), axis=0))...  9.98 us
    all_to_all x1, waiting for transfers between devices, on_device(): lax.all_to_all(yhat.reshape(1, 2, 2, cells), 'tm', split_axis=3, concat_a...  7.49 us
    all_to_all x1, waiting for transfers between devices, on_device(): lax.all_to_all(stacked, 'tm', split_axis=0, concat_axis=3, tiled=True)  7.25 us
  transfers between devices with their start and end apart: 11, of which 6 were waited for; matrix products, arithmetic and copies ran while one was open for 0% of the time, Pallas kernels for 0%

profile of v1, /device:TPU:0, one launch (start us, length us, event | category | flops | bytes accessed | tf_op | source)
XLA Modules:
  0.0 169.9 jit_solution(18304846746218273440)
XLA Ops:
  2.6 19.4 %reduce.68 = f32[4096,2]{1,0:T(8,128)} reduce(f32[4096,1,2]{2,1,0:T(1,128)S(1)} %bitcast.81, f32[]{:T(128)} %broadcast.187), dimensions={1}, to_apply=%bitcast.63.reduce_sub_computation | reduce | bytes 65540
  22.0 3.0 %reshape.251 = f32[16,1,512]{2,1,0:T(1,128)S(1)} reshape(f32[4096,2]{1,0:T(8,128)} %reduce.68) | data formatting | bytes 65536
  25.0 15.5 %all_to_all.53 = f32[16,1,512]{2,1,0:T(1,128)S(1)} all-to-all(f32[16,1,512]{2,1,0:T(1,128)S(1)} %reshape.251), channel_id=1, replica_groups=mesh['tm'=16,'rows'=2] {'tm'}, dimensions={0} | all-to-all | bytes 65536 | tf_op jit(solution)/shard_map/all_to_all | solution.py:61
  41.3 3.4 %reshape.252 = f32[4096,1,2]{2,1,0:T(1,128)S(1)} reshape(f32[16,512]{1,0:T(8,128)S(1)} %reduce.69) | data formatting | bytes 65536
  46.5 3.5 %all-to-all-start.1 = ((f32[16,2,2,256]{3,2,1,0:T(2,128)}), f32[16,2,2,256]{3,2,1,0:T(2,128)S(1)}, u32[]{:S(2)}, u32[]{:S(2)}) async-start(f32[16,2,2,256]{3,2,1,0:T(2,128)} %copy.48), calls=%async_computation.1 | async-start | bytes 131072 | tf_op jit(solution)/shard_map/all_to_all | solution.py:68
  50.3 7.2 %all-to-all-done.1 = f32[16,2,2,256]{3,2,1,0:T(2,128)S(1)} async-done(((f32[16,2,2,256]{3,2,1,0:T(2,128)}), f32[16,2,2,256]{3,2,1,0:T(2,128)S(1)}, u32[]{:S(2)}, u32[]{:S(2)}) %all-to-all-start.1) | async-done | bytes 65568 | tf_op jit(solution)/shard_map/all_to_all | solution.py:68
  57.6 1.3 collective-permute-start
  58.9 3.0 %collective-permute-start.1 = (f32[2,1,512]{2,1,0:T(1,128)S(1)}, f32[2,1,512]{2,1,0:T(1,128)S(1)}, u32[]{:S(2)}, u32[]{:S(2)}) collective-permute-start(f32[2,1,512]{2,1,0:T(1,128)S(1)} %get-tuple-element.42), channel_id=1, source_target_pairs={{0,1},{2,3},{4,5},{6,7},{8,9},{10,11},{12,13},{14,15},{16,17},{18,... | collective-permute-start | bytes 12296 | tf_op jit(solution)/shard_map/ppermute | solution.py:18
  62.9 1.3 collective-permute-start.2
  64.2 3.0 %collective-permute-start.3 = (f32[2,1,512]{2,1,0:T(1,128)S(1)}, f32[2,1,512]{2,1,0:T(1,128)S(1)}, u32[]{:S(2)}, u32[]{:S(2)}) collective-permute-start(f32[2,1,512]{2,1,0:T(1,128)S(1)} %get-tuple-element.38), channel_id=1, source_target_pairs={{0,1},{2,3},{4,5},{6,7},{8,9},{10,11},{12,13},{14,15},{16,17},{18,... | collective-permute-start | bytes 12296 | tf_op jit(solution)/shard_map/ppermute | solution.py:18
  68.1 1.3 collective-permute-start.4
  69.4 3.2 %collective-permute-start.5 = (f32[2,1,512]{2,1,0:T(1,128)S(1)}, f32[2,1,512]{2,1,0:T(1,128)S(1)}, u32[]{:S(2)}, u32[]{:S(2)}) collective-permute-start(f32[2,1,512]{2,1,0:T(1,128)S(1)} %get-tuple-element.34), channel_id=1, source_target_pairs={{0,1},{2,3},{4,5},{6,7},{8,9},{10,11},{12,13},{14,15},{16,17},{18,... | collective-permute-start | bytes 12296 | tf_op jit(solution)/shard_map/ppermute | solution.py:18
  73.5 4.4 %copy.51 = f32[1,2,2,4096]{2,1,0,3:T(2,128)} copy(f32[1,2,2,4096]{3,1,2,0:T(2,128)S(1)} %pad_maximum_fusion.1) | data formatting | bytes 131072 | tf_op jit(solution)/shard_map/stack | solution.py:86
  77.9 8.1 %reshape.253 = f32[16,1,1024]{2,1,0:T(1,128)} reshape(f32[4096,1,2,2]{3,2,1,0:T(2,128)} %bitcast.79) | data formatting | bytes 131072
  86.1 3.5 %all-to-all-start.2 = ((f32[16,1,1024]{2,1,0:T(1,128)}), f32[16,1,1024]{2,1,0:T(1,128)S(1)}, u32[]{:S(2)}, u32[]{:S(2)}) async-start(f32[16,1,1024]{2,1,0:T(1,128)} %reshape.253), calls=%async_computation.2 | async-start | bytes 131072 | tf_op jit(solution)/shard_map/all_to_all | solution.py:87
  89.6 7.5 %all-to-all-done.2 = f32[16,1,1024]{2,1,0:T(1,128)S(1)} async-done(((f32[16,1,1024]{2,1,0:T(1,128)}), f32[16,1,1024]{2,1,0:T(1,128)S(1)}, u32[]{:S(2)}, u32[]{:S(2)}) %all-to-all-start.2) | async-done | bytes 65568 | tf_op jit(solution)/shard_map/all_to_all | solution.py:87
  97.9 7.7 %reshape.254 = f32[4096,1,2,2]{3,2,1,0:T(2,128)} reshape(f32[16,1024]{1,0:T(8,128)S(1)} %reduce.70) | data formatting | bytes 131072
  105.6 3.6 %copy.57 = f32[1,2,2,16,256]{4,3,2,1,0:T(8,128)S(1)} copy(f32[1,2,2,16,256]{2,1,4,3,0:T(2,128)} %bitcast.80) | data formatting | bytes 131072 | tf_op jit(solution)/shard_map/all_to_all | solution.py:87
  110.2 10.0 %all_to_all.54 = f32[16,1,2,256]{3,2,1,0:T(2,128)S(1)} all-to-all(f32[16,1,2,256]{3,2,1,0:T(2,128)S(1)} %constant_dynamic-update-slice_fusion), channel_id=1, replica_groups=mesh['tm'=16,'rows'=2] {'tm'}, dimensions={0} | all-to-all | bytes 65536 | tf_op jit(solution)/shard_map/all_to_all | solution.py:98
  120.3 2.6 %collective-permute-start.6 = (f32[2,8,512]{2,1,0:T(8,128)S(1)}, f32[2,8,512]{2,1,0:T(8,128)S(1)}, u32[]{:S(2)}, u32[]{:S(2)}) collective-permute-start(f32[2,8,512]{2,1,0:T(8,128)S(1)} %reshape_squeeze_reshape.3), channel_id=1, source_target_pairs={{0,2},{2,4},{4,6},{6,8},{8,10},{10,12},{12,14},{14,16},{16,18},{18... | collective-permute-start | bytes 98312 | tf_op jit(solution)/shard_map/ppermute | solution.py:27
  122.9 1.3 collective-permute-start.7
  124.2 3.0 %collective-permute-start.8 = (f32[1,1,512]{2,1,0:T(1,128)S(1)}, f32[1,1,512]{2,1,0:T(1,128)S(1)}, u32[]{:S(2)}, u32[]{:S(2)}) collective-permute-start(f32[1,1,512]{2,1,0:T(1,128)S(1)} %get-tuple-element.46), channel_id=1, source_target_pairs={{0,1},{2,3},{4,5},{6,7},{8,9},{10,11},{12,13},{14,15},{16,17},{18,... | collective-permute-start | bytes 6152 | tf_op jit(solution)/shard_map/ppermute | solution.py:18
  128.2 1.2 pad_maximum_fusion.18
  130.9 39.0 %psum.7 = f32[5]{0:T(128)} all-reduce(f32[5]{0:T(128)S(1)} %pad_maximum_fusion.21), channel_id=1, replica_groups=mesh['tm'=16,'rows'=2] {'tm','rows'}, use_global_device_ids=true, to_apply=%region_2.3 | all-reduce | flops 5 | bytes 40 | tf_op jit(solution)/shard_map/psum | solution.py:112
  (98 shorter events, 10.7 us)
Async XLA Ops:
  46.5 11.0 %all-to-all-start.1 = ((f32[16,2,2,256]{3,2,1,0:T(2,128)}), f32[16,2,2,256]{3,2,1,0:T(2,128)S(1)}, u32[]{:S(2)}, u32[]{:S(2)}) async-start(f32[16,2,2,256]{3,2,1,0:T(2,128)} %copy.48), calls=%async_computation.1 | async-start | bytes 131072 | tf_op jit(solution)/shard_map/all_to_all | solution.py:68
  57.6 4.3 %collective-permute-start = (f32[2,1,512]{2,1,0:T(1,128)S(1)}, f32[2,1,512]{2,1,0:T(1,128)S(1)}, u32[]{:S(2)}, u32[]{:S(2)}) collective-permute-start(f32[2,1,512]{2,1,0:T(1,128)S(1)} %get-tuple-element.41), channel_id=1, source_target_pairs={{1,0},{3,2},{5,4},{7,6},{9,8},{11,10},{13,12},{15,14},{17,16},{19,... | collective-permute-start | bytes 12296 | tf_op jit(solution)/shard_map/ppermute | solution.py:19
  58.9 3.8 %collective-permute-start.1 = (f32[2,1,512]{2,1,0:T(1,128)S(1)}, f32[2,1,512]{2,1,0:T(1,128)S(1)}, u32[]{:S(2)}, u32[]{:S(2)}) collective-permute-start(f32[2,1,512]{2,1,0:T(1,128)S(1)} %get-tuple-element.42), channel_id=1, source_target_pairs={{0,1},{2,3},{4,5},{6,7},{8,9},{10,11},{12,13},{14,15},{16,17},{18,... | collective-permute-start | bytes 12296 | tf_op jit(solution)/shard_map/ppermute | solution.py:18
  62.9 4.3 %collective-permute-start.2 = (f32[2,1,512]{2,1,0:T(1,128)S(1)}, f32[2,1,512]{2,1,0:T(1,128)S(1)}, u32[]{:S(2)}, u32[]{:S(2)}) collective-permute-start(f32[2,1,512]{2,1,0:T(1,128)S(1)} %get-tuple-element.37), channel_id=1, source_target_pairs={{1,0},{3,2},{5,4},{7,6},{9,8},{11,10},{13,12},{15,14},{17,16},{19,... | collective-permute-start | bytes 12296 | tf_op jit(solution)/shard_map/ppermute | solution.py:19
  64.2 3.8 %collective-permute-start.3 = (f32[2,1,512]{2,1,0:T(1,128)S(1)}, f32[2,1,512]{2,1,0:T(1,128)S(1)}, u32[]{:S(2)}, u32[]{:S(2)}) collective-permute-start(f32[2,1,512]{2,1,0:T(1,128)S(1)} %get-tuple-element.38), channel_id=1, source_target_pairs={{0,1},{2,3},{4,5},{6,7},{8,9},{10,11},{12,13},{14,15},{16,17},{18,... | collective-permute-start | bytes 12296 | tf_op jit(solution)/shard_map/ppermute | solution.py:18
  68.1 4.5 %collective-permute-start.4 = (f32[2,1,512]{2,1,0:T(1,128)S(1)}, f32[2,1,512]{2,1,0:T(1,128)S(1)}, u32[]{:S(2)}, u32[]{:S(2)}) collective-permute-start(f32[2,1,512]{2,1,0:T(1,128)S(1)} %get-tuple-element.33), channel_id=1, source_target_pairs={{1,0},{3,2},{5,4},{7,6},{9,8},{11,10},{13,12},{15,14},{17,16},{19,... | collective-permute-start | bytes 12296 | tf_op jit(solution)/shard_map/ppermute | solution.py:19
  69.4 3.8 %collective-permute-start.5 = (f32[2,1,512]{2,1,0:T(1,128)S(1)}, f32[2,1,512]{2,1,0:T(1,128)S(1)}, u32[]{:S(2)}, u32[]{:S(2)}) collective-permute-start(f32[2,1,512]{2,1,0:T(1,128)S(1)} %get-tuple-element.34), channel_id=1, source_target_pairs={{0,1},{2,3},{4,5},{6,7},{8,9},{10,11},{12,13},{14,15},{16,17},{18,... | collective-permute-start | bytes 12296 | tf_op jit(solution)/shard_map/ppermute | solution.py:18
  86.1 11.0 %all-to-all-start.2 = ((f32[16,1,1024]{2,1,0:T(1,128)}), f32[16,1,1024]{2,1,0:T(1,128)S(1)}, u32[]{:S(2)}, u32[]{:S(2)}) async-start(f32[16,1,1024]{2,1,0:T(1,128)} %reshape.253), calls=%async_computation.2 | async-start | bytes 131072 | tf_op jit(solution)/shard_map/all_to_all | solution.py:87
  105.6 24.4 %copy-start = (f32[4,2,1,8,512]{4,3,2,1,0:T(8,128)S(1)}, f32[4,2,1,8,512]{4,3,2,1,0:T(8,128)}, u32[]{:S(2)}) copy-start(f32[4,2,1,8,512]{4,3,2,1,0:T(8,128)} %param.3) | copy-start | bytes 393220
  120.3 7.8 %collective-permute-start.6 = (f32[2,8,512]{2,1,0:T(8,128)S(1)}, f32[2,8,512]{2,1,0:T(8,128)S(1)}, u32[]{:S(2)}, u32[]{:S(2)}) collective-permute-start(f32[2,8,512]{2,1,0:T(8,128)S(1)} %reshape_squeeze_reshape.3), channel_id=1, source_target_pairs={{0,2},{2,4},{4,6},{6,8},{8,10},{10,12},{12,14},{14,16},{16,18},{18... | collective-permute-start | bytes 98312 | tf_op jit(solution)/shard_map/ppermute | solution.py:27
  122.9 4.4 %collective-permute-start.7 = (f32[1,1,512]{2,1,0:T(1,128)S(1)}, f32[1,1,512]{2,1,0:T(1,128)S(1)}, u32[]{:S(2)}, u32[]{:S(2)}) collective-permute-start(f32[1,1,512]{2,1,0:T(1,128)S(1)} %get-tuple-element.45), channel_id=1, source_target_pairs={{1,0},{3,2},{5,4},{7,6},{9,8},{11,10},{13,12},{15,14},{17,16},{19,... | collective-permute-start | bytes 6152 | tf_op jit(solution)/shard_map/ppermute | solution.py:19
  124.2 3.8 %collective-permute-start.8 = (f32[1,1,512]{2,1,0:T(1,128)S(1)}, f32[1,1,512]{2,1,0:T(1,128)S(1)}, u32[]{:S(2)}, u32[]{:S(2)}) collective-permute-start(f32[1,1,512]{2,1,0:T(1,128)S(1)} %get-tuple-element.46), channel_id=1, source_target_pairs={{0,1},{2,3},{4,5},{6,7},{8,9},{10,11},{12,13},{14,15},{16,17},{18,... | collective-permute-start | bytes 6152 | tf_op jit(solution)/shard_map/ppermute | solution.py:18
